TPU v7x, 32 devices: a whole 2x2x4 slice. The times are simulated.
32 devices in a mesh: frame: 8 (over y, x, core), row: 4 (over z).
Axes of the slice: x: 2, y: 2, z: 4, core: 2. Of those that a mesh axis runs over, the one named last changes fastest.
Arguments:
- tokens: bfloat16 [8, 512, 2048], P('frame', 'row'), may hold values from -6 to 6
- w_gate: bfloat16 [2048, 4096], P(None, 'row'), may hold values from -0.125 to 0.125
- w_value: bfloat16 [2048, 4096], P(None, 'row'), may hold values from -0.125 to 0.125
- w_state_proj: bfloat16 [2048, 512], replicated, may hold values from -0.03125 to 0.03125
- w_step: bfloat16 [2, 2048, 64], P(None, None, 'row'), may hold values from -0.125 to 0.125
- step_bias: float32 [2, 64], P(None, 'row'), may hold values from -3 to 0
- decay_rate: float32 [2, 64], P(None, 'row'), may hold values from 0 to 0.3, as said below
- conv_taps: float32 [2, 4, 4096], P(None, None, 'row'), may hold values from -3 to 3
- skip_gain: float32 [2, 64], P(None, 'row'), may hold values from 0.1 to 16, as said below
- norm_gain: float32 [4096], P('row'), may hold values from 0.1 to 1.9
- w_out: bfloat16 [4096, 2048], P('row'), may hold values from -0.09375 to 0.09375
Outputs:
- mixed: bfloat16 [8, 512, 2048], P('frame', 'row')
Inputs may be any that keep to these rules, and one draw needn't show every extreme that they name: `decay_rate`: positive decay rates. `skip_gain`: positive skip weights.
All inputs are finite; a program needn't handle non-finite values.
Results may differ from a plain program's by a relative error of at most 0.015.
Values may be sent and summed in bfloat16 or wider, within the bound.
No kernel may reach another device: no remote copies, remote signals or barrier semaphores. Data moves between devices by JAX's collectives and lax.ppermute only.
A program may use at most 128 MiB of HBM per device.

v0:
```python
import jax
import jax.numpy as jnp
from jax import lax
from jax.sharding import PartitionSpec as P

D_INNER = 4096
HEAD_DIM = 64
CONV = 4
BLK = 128


def with_halo(shard, sides, width):
    for axis, dim in sides:
        devices, length = (lax.axis_size(axis), shard.shape[dim])
        up = [(i, (i + 1) % devices) for i in range(devices - 1)]
        down = [(j, i) for i, j in up]
        last = lax.slice_in_dim(shard, length - width, length, axis=dim)
        initial = lax.slice_in_dim(shard, 0, width, axis=dim)
        before = lax.ppermute(last, axis, up)
        after = lax.ppermute(initial, axis, down)
        shard = jnp.concatenate([before, shard, after], axis=dim)
    return shard


def carried_in(shard, axis, combine, identity, reverse):
    devices, mine = (lax.axis_size(axis), lax.axis_index(axis))
    everything = jax.tree.map(
        lambda part, kind: lax.all_gather(part.astype(kind), axis),
        shard,
        (jnp.bfloat16, jnp.bfloat16),
    )
    start = jax.tree.map(
        lambda part, zero: jnp.broadcast_to(jnp.asarray(zero, part.dtype), part.shape),
        shard,
        identity,
    )

    def lap(k, before):
        at = devices - 1 - k if reverse else k
        reached = at > mine if reverse else at < mine
        new = combine(
            before, jax.tree.map(lambda part, own: part[at].astype(own.dtype), everything, shard)
        )
        return jax.tree.map(lambda a, b: jnp.where(reached, a, b), new, before)

    return lax.fori_loop(0, devices, lap, start)


def block_weights(scores, log_cum, dt_block):
    size = scores.shape[0]
    row_index = lax.broadcasted_iota(jnp.int32, (size, size), 0)
    col_index = lax.broadcasted_iota(jnp.int32, (size, size), 1)
    causal = row_index >= col_index
    log_gap = log_cum.T[:, :, None] - log_cum.T[:, None, :]
    fading = jnp.exp(jnp.where(causal[None], log_gap, -jnp.inf))
    return (scores[None] * fading * dt_block.T[:, None, :]).astype(jnp.bfloat16)


def local_pass(values, b_rows, c_rows, dt_rows, rate_row):
    tok_count, heads_here, head_width = values.shape
    block_count = tok_count // BLK
    blocks = (
        values.reshape(block_count, BLK, heads_here, head_width),
        b_rows.reshape(block_count, BLK, -1),
        c_rows.reshape(block_count, BLK, -1),
        dt_rows.reshape(block_count, BLK, heads_here),
    )
    state_zero = jnp.zeros((heads_here, head_width, b_rows.shape[1]), jnp.float32)

    def advance(carry, block):
        carry_state, offset = carry
        x_block, b_block, c_block, dt_block = block
        log_cum = jnp.cumsum(-dt_block * rate_row[None, :], axis=0)
        scores = jnp.einsum("tn,sn->ts", c_block, b_block, preferred_element_type=jnp.float32)
        weights = block_weights(scores, log_cum, dt_block)
        inner_out = jnp.einsum("hts,shp->thp", weights, x_block, preferred_element_type=jnp.float32)
        log_last = log_cum[-1]
        carried = (
            (jnp.exp(log_last[None, :] - log_cum) * dt_block)[:, :, None]
            * x_block.astype(jnp.float32)
        ).astype(jnp.bfloat16)
        update = jnp.einsum("sn,shp->hpn", b_block, carried, preferred_element_type=jnp.float32)
        new_state = jnp.exp(log_last)[:, None, None] * carry_state + update
        return ((new_state, offset + log_last), (inner_out, log_cum, carry_state, offset))

    finals, saved = lax.scan(advance, (state_zero, jnp.zeros((heads_here,), jnp.float32)), blocks)
    return (finals, saved, blocks)


def finish(saved, blocks, incoming, skip_row):
    inner_out, log_cum, starts, offsets = saved
    x_blocks, unused_b, c_blocks, unused_dt = blocks
    entering = (starts + jnp.exp(offsets)[:, :, None, None] * incoming[None]).astype(jnp.bfloat16)
    carried_out = jnp.einsum(
        "btn,bhpn->bthp", c_blocks, entering, preferred_element_type=jnp.float32
    )
    result = (
        inner_out
        + carried_out * jnp.exp(log_cum)[..., None]
        + skip_row[None, None, :, None] * x_blocks.astype(jnp.float32)
    )
    return result.reshape(-1, result.shape[2], result.shape[3])


def chain_link(earlier, later):
    return (earlier[0] + later[0], jnp.exp(later[0])[:, None, None] * earlier[1] + later[1])


def conv_pass(padded, taps, tok_count, backward):
    reach = taps.shape[0] - 1
    running = jnp.zeros((tok_count, padded.shape[1]), jnp.float32)
    for tap_index in range(taps.shape[0]):
        first_row = 2 * reach - tap_index if backward else tap_index
        running = running + taps[tap_index][None, :] * padded[first_row : first_row + tok_count]
    return jax.nn.silu(running).astype(jnp.bfloat16)


def per_device(
    tokens,
    w_gate,
    w_value,
    w_state_proj,
    w_step,
    step_bias,
    decay_rate,
    conv_taps,
    skip_gain,
    norm_gain,
    w_out,
):
    channels = w_gate.shape[1]
    heads_here = step_bias.shape[1]
    state_size = w_state_proj.shape[1] // 4
    shard_piece = lax.all_gather(tokens, "row", axis=1, tiled=True)
    matrices = (w_gate, w_value, w_state_proj, w_step[0], w_step[1])
    outputs = [
        jnp.einsum("frd,dk->frk", shard_piece, matrix, preferred_element_type=jnp.float32).astype(
            jnp.bfloat16
        )
        for matrix in matrices
    ]
    projected = jnp.concatenate(outputs, axis=2)
    frame_count, patch_count = (projected.shape[0], projected.shape[1])
    tok_count = frame_count * patch_count
    projected = projected.reshape(tok_count, -1)
    gate_in = projected[:, :channels]
    x_raw = projected[:, channels : 2 * channels]
    edge = 2 * channels + 4 * state_size
    bc_cols = projected[:, 2 * channels : edge]
    dt_forward = jax.nn.softplus(
        projected[:, edge : edge + heads_here].astype(jnp.float32) + step_bias[0][None, :]
    )
    dt_backward = jax.nn.softplus(
        projected[:, edge + heads_here : edge + 2 * heads_here].astype(jnp.float32)
        + step_bias[1][None, :]
    )
    padded = with_halo(x_raw, (("frame", 0),), CONV - 1).astype(jnp.float32)
    shape_heads = (tok_count, heads_here, HEAD_DIM)
    x_forward = conv_pass(padded, conv_taps[0], tok_count, False).reshape(shape_heads)
    x_backward = conv_pass(padded, conv_taps[1], tok_count, True).reshape(shape_heads)
    finals_fwd, saved_fwd, blocks_fwd = local_pass(
        x_forward,
        bc_cols[:, :state_size],
        bc_cols[:, state_size : 2 * state_size],
        dt_forward,
        decay_rate[0],
    )
    finals_bwd, saved_bwd, blocks_bwd = local_pass(
        jnp.flip(x_backward, 0),
        jnp.flip(bc_cols[:, 2 * state_size : 3 * state_size], 0),
        jnp.flip(bc_cols[:, 3 * state_size :], 0),
        jnp.flip(dt_backward, 0),
        decay_rate[1],
    )
    empty_pair = (
        jnp.zeros((heads_here,), jnp.float32),
        jnp.zeros((heads_here, HEAD_DIM, state_size), jnp.float32),
    )
    entry_fwd = carried_in((finals_fwd[1], finals_fwd[0]), "frame", chain_link, empty_pair, False)[
        1
    ]
    entry_bwd = carried_in((finals_bwd[1], finals_bwd[0]), "frame", chain_link, empty_pair, True)[1]
    y_forward = finish(saved_fwd, blocks_fwd, entry_fwd, skip_gain[0])
    y_backward = jnp.flip(finish(saved_bwd, blocks_bwd, entry_bwd, skip_gain[1]), 0)
    summed = (y_forward + y_backward).reshape(tok_count, channels)
    gated = summed * jax.nn.silu(gate_in.astype(jnp.float32))
    local_squares = jnp.sum(gated * gated, axis=-1)
    total_squares = lax.psum(local_squares, "row")
    scale = lax.rsqrt(total_squares / D_INNER + 1e-05)
    normed = (gated * scale[:, None] * norm_gain[None, :]).astype(jnp.bfloat16)
    normed = normed.reshape(frame_count, patch_count, channels)
    partial_value = jnp.einsum("fpc,cd->fpd", normed, w_out, preferred_element_type=jnp.float32)
    reduced = lax.psum_scatter(
        jnp.transpose(partial_value, (1, 0, 2)).astype(jnp.bfloat16),
        "row",
        scatter_dimension=0,
        tiled=True,
    ).astype(jnp.float32)
    mixed = jnp.transpose(reduced, (1, 0, 2)).astype(jnp.bfloat16)
    return mixed


def solution(mesh):
    return jax.shard_map(
        per_device,
        mesh=mesh,
        in_specs=(
            P("frame", "row", None),
            P(None, "row"),
            P(None, "row"),
            P(),
            P(None, None, "row"),
            P(None, "row"),
            P(None, "row"),
            P(None, None, "row"),
            P(None, "row"),
            P("row"),
            P("row", None),
        ),
        out_specs=P("frame", "row", None),
        check_vma=False,
    )
```

profile of v0, /device:TPU:0, one launch (start us, length us, event | category | flops | bytes accessed | tf_op | source)
XLA Modules:
  0.0 298.6 jit_solution(7827594384585309129)
XLA Ops:
  8.1 1.3 fusion.140
  9.5 1.5 fusion.139
  11.0 46.3 %all-gather.8.cloned.1.call-done = bf16[1,512,2048]{2,1,0:T(8,128)(2,1)} async-done(((bf16[1,128,2048]{2,1,0:T(8,128)(2,1)}), bf16[1,512,2048]{2,1,0:T(8,128)(2,1)}) %all-gather.8.cloned.1.call-update) | async-done | bytes 2097168 | tf_op jit(solution)/shard_map/all_gather | solution.py:134
  57.3 5.3 %fusion.94 = bf16[1,512,2592]{1,2,0:T(8,128)(2,1)S(1)} fusion(bf16[2048,1024]{1,0:T(8,128)(2,1)} %param.20, bf16[1,512,2048]{2,1,0:T(8,128)(2,1)} %all-gather.8.cloned.1.call-done), kind=kOutput, calls=%fused_computation.129 | convolution fusion | flops 2148007936 | bytes 7340032 | tf_op jit(solution)/shard_map/frd,dk->frk/dot_general | solution.py:137
  62.7 2.4 fusion.88
  65.1 1.3 fusion.103
  69.5 1.3 collective-permute-start.1
  70.8 3.7 %collective-permute-start = (bf16[3,1024]{0,1:T(8,128)(2,1)}, bf16[3,1024]{0,1:T(8,128)(2,1)}, u32[]{:S(2)}, u32[]{:S(2)}) collective-permute-start(bf16[3,1024]{0,1:T(8,128)(2,1)} %get-tuple-element.661), channel_id=1, source_target_pairs={{0,4},{4,8},{8,12},{12,16},{16,20},{20,24},{24,28},{1,5},{5,9},{9,... | collective-permute-start | bytes 18440 | tf_op jit(solution)/shard_map/ppermute | solution.py:19
  80.8 1.7 copy.102
  84.2 2.0 maximum_convert_fusion
  86.2 5.8 %multiply_convert_fusion.8 = (bf16[512,1024]{0,1:T(8,128)(2,1)}, bf16[512,1024]{0,1:T(8,128)(2,1)}) fusion(f32[518,1024]{0,1:T(8,128)S(1)} %maximum_convert_fusion, f32[1024]{0:T(1024)S(1)} %bitcast.313, f32[1024]{0:T(1024)S(1)} %bitcast.314, f32[1024]{0:T(1024)S(1)} %bitcast.315, f32[1024]{0:T(1024)S(1)} %bitcast.310, f32[1024]{0:T(1024)S(1)} %bitcast.316, ...), kind=kLoop, calls=%fused_computation.123 | loop fusion | flops 12582912 | bytes 16809984 | tf_op jit(solution)/shard_map/convert_element_type | solution.py:115
  92.0 3.7 %rev.20 = bf16[512,16,64]{0,2,1:T(8,128)(2,1)} reverse(bf16[512,16,64]{0,2,1:T(8,128)(2,1)} %bitcast.297), dimensions={0} | reverse | bytes 2097152 | tf_op jit(solution)/shard_map/jit(_flip)/rev | solution.py:169
  95.6 2.5 copy_bitcast_fusion.1
  98.1 1.6 broadcast.55.clone
  100.5 1.6 broadcast.57.clone
  102.6 44.9 %while.74 = (s32[]{:T(128)}, f32[16,64,128]{2,1,0:T(8,128)S(1)}, f32[16]{0:T(128)}, f32[4,128,16,64]{1,3,2,0:T(8,128)}, f32[4,128,16]{2,1,0:T(8,128)}, /*index=5...) while((s32[]{:T(128)}, f32[16,64,128]{2,1,0:T(8,128)S(1)}, ...), condition=%wide.region_7.8_spmd.clone, body=%wide.region_5.7_spmd.clone.sunk | while | flops 73816096 | bytes 3641788 | solution.py:86
  106.0 1.2 convolution_add_fusion.5
  109.1 2.3 fusion.185
  112.1 1.3 dynamic_update_slice.57
  116.1 1.2 fusion.183
  117.3 1.2 convolution_add_fusion.5
  120.5 2.3 fusion.185
  123.4 1.3 dynamic_update_slice.57
  127.5 1.2 fusion.183
  128.7 1.2 convolution_add_fusion.5
  131.9 2.3 fusion.185
  134.8 1.3 dynamic_update_slice.57
  138.9 1.2 fusion.183
  140.1 1.2 convolution_add_fusion.5
  143.3 2.4 fusion.185
  146.2 1.3 dynamic_update_slice.57
  147.5 2.1 reshape_reshape.3
  149.6 2.5 copy.82
  153.0 1.7 broadcast.55.clone.1
  154.7 1.6 broadcast.57.clone.1
  156.3 23.3 %while.72 = (s32[]{:T(128)}, f32[16,64,128]{2,1,0:T(8,128)S(1)}, f32[16]{0:T(128)S(1)}, f32[4,128,16,64]{1,3,2,0:T(8,128)}, f32[4,128,16]{2,1,0:T(8,128)S(1)}, /...) while((s32[]{:T(128)}, f32[16,64,128]{2,1,0:T(8,128)S(1)}, ...), condition=%wide.region_2.3_spmd.clone, body=%wide.region_0.2_spmd.clone.sunk | while | flops 73816096 | bytes 3699580 | solution.py:86
  157.4 1.2 convolution_add_fusion.4
  159.7 2.3 fusion.175
  163.2 1.2 convolution_add_fusion.4
  165.5 2.3 fusion.175
  169.0 1.2 convolution_add_fusion.4
  171.3 2.3 fusion.175
  174.9 1.2 convolution_add_fusion.4
  177.2 2.3 fusion.175
  180.5 1.3 dynamic-slice
  184.7 13.4 %all-reduce.2 = (bf16[128]{0:T(256)(128)(2,1)S(1)}, bf16[128]{0:T(256)(128)(2,1)S(1)}) all-reduce(bf16[128]{0:T(256)(128)(2,1)S(1)} %dynamic-update-slice.1, bf16[128]{0:T(256)(128)(2,1)S(1)} %dynamic-update-slice), channel_id=4, replica_groups=mesh['frame'=8,'row'=4] {'frame'}, use_global_device_ids=true, to_apply=%add.1 | all-reduce | flops 256 | bytes 1024
  199.4 9.2 %while.75 = (s32[]{:T(128)}, f32[16,64,128]{2,1,0:T(8,128)S(1)}, s32[]{:T(128)}, bf16[8,16]{1,0:T(8,128)(2,1)S(1)}, bf16[8,16,64,128]{3,2,1,0:T(8,128)(2,1)}, /*index=5*/s32[]{:T(128)}, s32[]{:T(128)}, s32[]{:T(128)}, s32[]{:T(128)}) while((s32[]{:T(128)}, f32[16,64,128]{2,1,0:T(8,128)S(1)}, s32[]{:T(128)}, ...), condition=%wide.region_9.10_spmd.clone, body=%wide.region_8.9_spmd.clone.sunk | while | flops 655384 | bytes 1311055 | solution.py:46
  199.4 1.1 fusion.186
  200.6 1.1 fusion.186
  201.7 1.1 fusion.186
  204.0 1.1 fusion.186
  205.2 1.1 fusion.186
  208.6 3.1 %add_bitcast_fusion = f32[4,16,8,8,128]{4,3,2,1,0:T(8,128)S(1)} fusion(f32[4,128,16,64]{1,3,2,0:T(8,128)} %get-tuple-element.372, f32[4,16,64,128]{3,2,1,0:T(8,128)} %get-tuple-element.373, f32[16]{0:T(128)S(1)} %get-tuple-element.674, f32[4,128,16]{1,2,0:T(8,128)S(1)} %copy.94, f32[16,64,128]{2,1,0:T(8,128)S(1)} %get-tuple-element.377, ...), kind=kOutput, calls=%fused_computation.118 | convolution fusion | flops 138412032 | bytes 8028480 | tf_op jit(solution)/shard_map/btn,bhpn->bthp/dot_general | solution.py:94
  211.7 1.7 copy.122
  213.4 4.2 %rev.23 = f32[512,16,64]{0,2,1:T(8,128)} reverse(f32[512,16,64]{0,2,1:T(8,128)} %bitcast.294), dimensions={0} | reverse | bytes 4194304 | tf_op jit(solution)/shard_map/jit(_flip)/rev | solution.py:184
  217.6 9.1 %while.73 = (s32[]{:T(128)}, f32[16,64,128]{2,1,0:T(8,128)S(1)}, s32[]{:T(128)}, bf16[8,16]{1,0:T(8,128)(2,1)S(1)}, bf16[8,16,64,128]{3,2,1,0:T(8,128)(2,1)}, /*index=5*/s32[]{:T(128)}, s32[]{:T(128)}) while((s32[]{:T(128)}, f32[16,64,128]{2,1,0:T(8,128)S(1)}, s32[]{:T(128)}, bf16[8,16]{1,0:T(8,128)(2,1)S(1)}, ...), condition=%wide.region_4.5_spmd.clone, body=%wide.region_3.4_spmd.clone.sunk | while | flops 655380 | bytes 1310993 | solution.py:46
  217.6 1.1 fusion.176
  218.7 1.1 fusion.176
  221.0 1.1 fusion.176
  226.7 3.3 %add_bitcast_fusion.1 = f32[4,16,8,8,128]{4,3,2,1,0:T(8,128)S(1)} fusion(f32[4,128,16,64]{1,3,2,0:T(8,128)} %get-tuple-element.365, f32[4,16,64,128]{3,2,1,0:T(8,128)} %get-tuple-element.366, f32[16]{0:T(128)S(1)} %get-tuple-element.673, f32[4,128,16]{1,2,0:T(8,128)S(1)} %copy.86, f32[16,64,128]{2,1,0:T(8,128)S(1)} %get-tuple-element.370, ...), kind=kOutput, calls=%fused_computation.121 | convolution fusion | flops 138412032 | bytes 8028480 | tf_op jit(solution)/shard_map/btn,bhpn->bthp/dot_general | solution.py:94
  230.3 3.2 %multiply_reduce_fusion = (f32[512]{0:T(512)S(1)}, f32[512,1024]{0,1:T(8,128)}) fusion(bf16[512,2592]{0,1:T(8,128)(2,1)} %bitcast.302, f32[512,16,64]{0,2,1:T(8,128)S(1)} %bitcast_add_fusion), kind=kLoop, calls=%fused_computation.117 | loop fusion | flops 4193792 | bytes 5244928 | tf_op jit(solution)/shard_map/reduce_sum | solution.py:187
  233.6 9.6 %psum.7 = f32[512]{0:T(512)S(1)} all-reduce(f32[512]{0:T(512)S(1)} %get-tuple-element.647), channel_id=1, replica_groups=mesh['frame'=8,'row'=4] {'row'}, use_global_device_ids=true, to_apply=%region_11.12 | all-reduce | flops 512 | bytes 4096 | tf_op jit(solution)/shard_map/psum | solution.py:188
  243.2 6.7 %fusion.58 = bf16[512,1,2048]{2,0,1:T(8,128)(2,1)} fusion(bf16[1024,2048]{1,0:T(8,128)(2,1)} %param.29, f32[512,1024]{0,1:T(8,128)} %get-tuple-element.648, f32[1024]{0:T(1024)S(1)} %copy-done.20, f32[512]{0:T(512)S(1)} %add_rsqrt_fusion), kind=kOutput, calls=%fused_computation.85 | convolution fusion | flops 2150105088 | bytes 8394752 | tf_op jit(solution)/shard_map/fpc,cd->fpd/dot_general | solution.py:192
  249.9 42.1 %reduce-scatter.2.cloned.1.call-done = bf16[128,1,2048]{2,0,1:T(8,128)(2,1)} async-done(((bf16[512,1,2048]{2,0,1:T(8,128)(2,1)}), bf16[128,1,2048]{2,0,1:T(8,128)(2,1)}) %reduce-scatter.2.cloned.1.call-update) | async-done | bytes 524304 | tf_op jit(solution)/shard_map/reduce_scatter | solution.py:193
  (229 shorter events, 59.4 us)
Async XLA Ops:
  6.5 58.6 %copy-start = (bf16[2048,512]{1,0:T(8,128)(2,1)S(1)}, bf16[2048,512]{1,0:T(8,128)(2,1)}, u32[]{:S(2)}) copy-start(bf16[2048,512]{1,0:T(8,128)(2,1)} %param.22) | copy-start | bytes 6291460
  6.5 50.8 %all-gather.8.cloned.1.call-start = ((), (), s32[]{:S(2)}) async-start(), calls=%async_computation.1 | async-start | bytes 2621440 | tf_op jit(solution)/shard_map/all_gather | solution.py:134
  7.3 192.1 %all-gather.12.cloned.1.call-start = ((), (), s32[]{:S(2)}) async-start(), calls=%async_computation.4 | async-start | bytes 2359296 | tf_op jit(solution)/shard_map/all_gather | solution.py:28
  57.3 5.4 %copy-start.2 = (bf16[1,512,2048]{2,1,0:T(8,128)(2,1)S(1)}, bf16[1,512,2048]{2,1,0:T(8,128)(2,1)}, u32[]{:S(2)}) copy-start(bf16[1,512,2048]{2,1,0:T(8,128)(2,1)} %all-gather.8.cloned.1.call-done) | copy-start | bytes 6291460
  57.3 5.4 %copy-start.19 = (bf16[2048,1024]{1,0:T(8,128)(2,1)S(1)}, bf16[2048,1024]{1,0:T(8,128)(2,1)}, u32[]{:S(2)}) copy-start(bf16[2048,1024]{1,0:T(8,128)(2,1)} %param.21) | copy-start | bytes 12582916
  65.1 1.3 copy-start.10
  67.7 8.6 %copy-start.3 = (bf16[1,512,2592]{1,2,0:T(8,128)(2,1)}, bf16[1,512,2592]{1,2,0:T(8,128)(2,1)S(1)}, u32[]{:S(2)}) copy-start(bf16[1,512,2592]{1,2,0:T(8,128)(2,1)S(1)} %fusion.115) | copy-start | bytes 7962628
  69.5 14.7 %collective-permute-start.1 = (bf16[3,1024]{0,1:T(8,128)(2,1)}, bf16[3,1024]{0,1:T(8,128)(2,1)}, u32[]{:S(2)}, u32[]{:S(2)}) collective-permute-start(bf16[3,1024]{0,1:T(8,128)(2,1)} %get-tuple-element.662), channel_id=1, source_target_pairs={{4,0},{8,4},{12,8},{16,12},{20,16},{24,20},{28,24},{5,1},{9,5},{13... | collective-permute-start | bytes 18440 | tf_op jit(solution)/shard_map/ppermute | solution.py:20
  70.8 13.4 %collective-permute-start = (bf16[3,1024]{0,1:T(8,128)(2,1)}, bf16[3,1024]{0,1:T(8,128)(2,1)}, u32[]{:S(2)}, u32[]{:S(2)}) collective-permute-start(bf16[3,1024]{0,1:T(8,128)(2,1)} %get-tuple-element.661), channel_id=1, source_target_pairs={{0,4},{4,8},{8,12},{12,16},{16,20},{20,24},{24,28},{1,5},{5,9},{9,... | collective-permute-start | bytes 18440 | tf_op jit(solution)/shard_map/ppermute | solution.py:19
  79.1 3.3 %copy-start.7 = (bf16[4,128,128]{1,0,2:T(4,128)(2,1)}, bf16[4,128,128]{1,0,2:T(4,128)(2,1)S(1)}, u32[]{:S(2)}) copy-start(bf16[4,128,128]{1,0,2:T(4,128)(2,1)S(1)} %reshape.213) | copy-start | bytes 393220
  83.4 2.8 copy-start.5
  84.2 2.0 copy-start.12
  84.2 2.0 copy-start.13
  84.2 2.0 copy-start.14
  84.2 2.0 copy-start.15
  152.9 64.7 %all-gather.10.cloned.1.call-start = ((), (), s32[]{:S(2)}) async-start(), calls=%async_computation.3 | async-start | bytes 2359296 | tf_op jit(solution)/shard_map/all_gather | solution.py:28
  152.9 3.3 %copy-start.4 = (bf16[512,128]{1,0:T(8,128)(2,1)S(1)}, bf16[512,128]{1,0:T(8,128)(2,1)}, u32[]{:S(2)}) copy-start(bf16[512,128]{1,0:T(8,128)(2,1)} %copy.102) | copy-start | bytes 393220
  153.0 3.3 %copy-start.11 = (f32[1,16]{1,0:T(1,128)S(1)}, f32[1,16]{1,0:T(1,128)}, u32[]{:S(2)}) copy-start(f32[1,16]{1,0:T(1,128)} %get-tuple-element.952) | copy-start | bytes 196
  153.0 3.3 %copy-start.16 = (f32[16]{0:T(128)S(1)}, f32[16]{0:T(128)}, u32[]{:S(2)}) copy-start(f32[16]{0:T(128)} %custom-call.1) | copy-start | bytes 196
  156.3 26.2 %copy-start.18 = (f32[2,16]{1,0:T(2,128)S(1)}, f32[2,16]{1,0:T(2,128)}, u32[]{:S(2)}) copy-start(f32[2,16]{1,0:T(2,128)} %param.27) | copy-start | bytes 388
  156.3 41.9 %copy-start.17 = (f32[4,16]{1,0:T(4,128)S(1)}, f32[4,16]{1,0:T(4,128)}, u32[]{:S(2)}) copy-start(f32[4,16]{1,0:T(4,128)} %get-tuple-element.374) | copy-start | bytes 772
  179.6 0.9 copy-start.9
  180.4 111.6 %reduce-scatter.2.cloned.1.call-start = ((), (), s32[]{:S(2)}) async-start(), calls=%async_computation.2 | async-start | bytes 2621440 | tf_op jit(solution)/shard_map/reduce_scatter | solution.py:193
  199.4 9.2 %copy-start.8 = (bf16[4,128,128]{1,0,2:T(4,128)(2,1)S(1)}, bf16[4,128,128]{1,0,2:T(4,128)(2,1)}, u32[]{:S(2)}) copy-start(bf16[4,128,128]{1,0,2:T(4,128)(2,1)} %copy-done.7) | copy-start | bytes 393220
  217.6 9.1 %copy-start.6 = (bf16[4,128,128]{1,0,2:T(4,128)(2,1)S(1)}, bf16[4,128,128]{1,0,2:T(4,128)(2,1)}, u32[]{:S(2)}) copy-start(bf16[4,128,128]{1,0,2:T(4,128)(2,1)} %copy-done.5) | copy-start | bytes 393220
  226.7 3.3 %copy-start.1 = (f32[512,16,64]{0,2,1:T(8,128)S(1)}, f32[512,16,64]{0,2,1:T(8,128)}, u32[]{:S(2)}) copy-start(f32[512,16,64]{0,2,1:T(8,128)} %rev.23) | copy-start | bytes 6291460
  230.3 12.9 %copy-start.20 = (f32[1024]{0:T(1024)S(1)}, f32[1024]{0:T(1024)}, u32[]{:S(2)}) copy-start(f32[1024]{0:T(1024)} %param.28) | copy-start | bytes 12292
Sparse Core Ops, SparseCore 0:
  8.9 48.3 all-gather.7
  153.0 26.8 all-gather.11
  181.8 27.8 all-gather.9
  250.0 41.9 reduce-scatter.1
where the time goes:
time: 302 us; the launch traced here: 299 us
  waiting for transfers between devices  89.3 us (30%)
  matrix products  58.9 us (20%)
  local copies, waits for them, and re-layouts  55.5 us (18%)
  other arithmetic  51.7 us (17%)
  blocking collectives  23 us (8%)
  between operations  14.2 us (5%)
  starting transfers between devices  5.15 us (2%)
    all_gather x1, waiting for transfers between devices, per_device(): shard_piece = lax.all_gather(tokens, 'row', axis=1, tiled=True)  46.3 us
    reduce_scatter x1, waiting for transfers between devices, per_device(): lax.psum_scatter(jnp.transpose(partial_value, (1, 0, 2)).astype(jnp.bfloa...  42.1 us
    dot_general x8, matrix products, advance(): jnp.einsum('hts,shp->thp', weights, x_block, preferred_element_type=jnp.f...  18.6 us
    select_n x16, other arithmetic, lap(): return jax.tree.map(lambda a, b: jnp.where(reached, a, b), new, before)  17.5 us
    unnamed x1, blocking collectives  13.4 us
    unnamed x55, local copies, waits for them, and re-layouts  12.5 us
    dot_general x5, matrix products, per_device(): jnp.einsum('frd,dk->frk', shard_piece, matrix, preferred_element_type=jnp...  10.4 us
    psum x1, blocking collectives, per_device(): total_squares = lax.psum(local_squares, 'row')  9.61 us
  transfers between devices with their start and end apart: 6, of which 2 were waited for; matrix products, arithmetic and copies ran while one was open for 21% of the time, Pallas kernels for 0%

commit v1 on v0

--- a/solution.py
+++ b/solution.py
@@ -131,7 +131,13 @@
     channels = w_gate.shape[1]
     heads_here = step_bias.shape[1]
     state_size = w_state_proj.shape[1] // 4
-    shard_piece = lax.all_gather(tokens, "row", axis=1, tiled=True)
+    count = lax.axis_size("row")
+    current, tiles = (tokens, [tokens])
+    for _ in range(count - 1):
+        current = lax.ppermute(current, "row", [(i_2, (i_2 + 1) % count) for i_2 in range(count)])
+        tiles.insert(0, current)
+    merged = jnp.concatenate(tiles, axis=1)
+    shard_piece = jnp.roll(merged, (lax.axis_index("row") + 1) * tokens.shape[1], axis=1)
     matrices = (w_gate, w_value, w_state_proj, w_step[0], w_step[1])
     outputs = [
         jnp.einsum("frd,dk->frk", shard_piece, matrix, preferred_element_type=jnp.float32).astype(

time: 302 us -> 260 us (0.86)
  local copies, waits for them, and re-layouts: 55.5 us -> 38.3 us
  other arithmetic: 51.7 us -> 39.2 us
  matrix products: 58.9 us -> 52.6 us
  waiting for transfers between devices: 89.3 us -> 83.2 us
  starting transfers between devices: 5.15 us -> 8.18 us
    all_gather x1 -> x0, waiting for transfers between devices: 46.3 us -> none  [per_device(): shard_piece = lax.all_gather(tokens, 'row', axis=1, tiled=True)]
    ppermute x0 -> x3, waiting for transfers between devices: none -> 40.3 us  [per_device(): lax.ppermute(current, 'row', [(i_2, (i_2 + 1) % count) for i_2 in range(c...]
    dynamic_update_slice x16, local copies, waits for them, and re-layouts: 7.74 us -> 0.38 us  [local_pass(): lax.scan(advance, (state_zero, jnp.zeros((heads_here,), jnp.float32)), bl...]
    add x8, other arithmetic: 4.33 us -> 0.1 us  [advance(): offset + log_last]
    transpose x16, local copies, waits for them, and re-layouts: 3.88 us -> 0.51 us  [block_weights(): return (scores[None] * fading * dt_block.T[:, None, :]).astype(jnp.bfloat16)]
    mul x8, other arithmetic: 3.42 us -> 0.06 us  [advance(): log_cum = jnp.cumsum(-dt_block * rate_row[None, :], axis=0)]
    mul x8, other arithmetic: 3.53 us -> 0.18 us  [advance(): jnp.exp(log_last[None, :] - log_cum) * dt_block]
    dot_general x8, matrix products: 7.37 us -> 4.22 us  [advance(): jnp.einsum('tn,sn->ts', c_block, b_block, preferred_element_type=jnp.floa...]
  transfers between devices with their start and end apart: 6 -> 8, of which waited for: 2 -> 4; matrix products, arithmetic and copies ran while one was open for 21% -> 21% of each run, Pallas kernels for 0% -> 0%
where the time goes in v1:
time: 260 us; the launch traced here: 258 us
  waiting for transfers between devices  83.2 us (32%)
  matrix products  52.6 us (20%)
  other arithmetic  39.2 us (15%)
  local copies, waits for them, and re-layouts  38.3 us (15%)
  blocking collectives  21.4 us (8%)
  between operations  14.3 us (6%)
  starting transfers between devices  8.18 us (3%)
    reduce_scatter x1, waiting for transfers between devices, per_device(): lax.psum_scatter(jnp.transpose(partial_value, (1, 0, 2)).astype(jnp.bfloa...  42.8 us
    ppermute x3, waiting for transfers between devices, per_device(): lax.ppermute(current, 'row', [(i_2, (i_2 + 1) % count) for i_2 in range(c...  40.3 us
    dot_general x8, matrix products, advance(): jnp.einsum('hts,shp->thp', weights, x_block, preferred_element_type=jnp.f...  18.7 us
    select_n x16, other arithmetic, lap(): return jax.tree.map(lambda a, b: jnp.where(reached, a, b), new, before)  17.6 us
    unnamed x1, blocking collectives  13 us
    unnamed x76, local copies, waits for them, and re-layouts  12.1 us
    dot_general x8, matrix products, advance(): jnp.einsum('sn,shp->hpn', b_block, carried, preferred_element_type=jnp.fl...  9.57 us
    psum x1, blocking collectives, per_device(): total_squares = lax.psum(local_squares, 'row')  8.34 us
  transfers between devices with their start and end apart: 8, of which 4 were waited for; matrix products, arithmetic and copies ran while one was open for 21% of the time, Pallas kernels for 0%

profile of v1, /device:TPU:0, one launch (start us, length us, event | category | flops | bytes accessed | tf_op | source)
XLA Modules:
  0.0 258.2 jit_solution(3260966323146290923)
XLA Ops:
  6.5 3.1 %collective-permute-start = (bf16[1,128,2048]{2,1,0:T(8,128)(2,1)}, bf16[1,128,2048]{2,1,0:T(8,128)(2,1)S(1)}, u32[]{:S(2)}, u32[]{:S(2)}) collective-permute-start(bf16[1,128,2048]{2,1,0:T(8,128)(2,1)} %param.19), channel_id=1, source_target_pairs={{0,1},{1,2},{2,3},{3,0},{4,5},{5,6},{6,7},{7,4},{8,9},{9,10},{10,1... | collective-permute-start | bytes 1572872 | tf_op jit(solution)/shard_map/ppermute | solution.py:137
  9.6 14.2 %collective-permute-done = bf16[1,128,2048]{2,1,0:T(8,128)(2,1)S(1)} collective-permute-done((bf16[1,128,2048]{2,1,0:T(8,128)(2,1)}, bf16[1,128,2048]{2,1,0:T(8,128)(2,1)S(1)}, u32[]{:S(2)}, u32[]{:S(2)}) %collective-permute-start) | collective-permute-done | bytes 524320 | tf_op jit(solution)/shard_map/ppermute | solution.py:137
  23.8 15.0 %collective-permute-done.1 = bf16[1,128,2048]{2,1,0:T(8,128)(2,1)} collective-permute-done((bf16[1,128,2048]{2,1,0:T(8,128)(2,1)S(1)}, bf16[1,128,2048]{2,1,0:T(8,128)(2,1)}, u32[]{:S(2)}, u32[]{:S(2)}) %collective-permute-start.1) | collective-permute-done | bytes 524320 | tf_op jit(solution)/shard_map/ppermute | solution.py:137
  40.3 1.5 fusion.149
  41.9 11.2 %collective-permute-done.2 = bf16[1,128,2048]{2,1,0:T(8,128)(2,1)} collective-permute-done((bf16[1,128,2048]{2,1,0:T(8,128)(2,1)}, bf16[1,128,2048]{2,1,0:T(8,128)(2,1)}, u32[]{:S(2)}, u32[]{:S(2)}) %collective-permute-start.2) | collective-permute-done | bytes 524320 | tf_op jit(solution)/shard_map/ppermute | solution.py:137
  55.4 1.2 constant_dynamic-update-slice_fusion.3
  56.6 1.2 constant_dynamic-update-slice_fusion.2
  58.0 2.4 fusion.94
  60.4 2.4 fusion.88
  62.8 1.3 fusion.103
  67.1 1.3 collective-permute-start.4
  68.4 3.8 %collective-permute-start.3 = (bf16[3,1024]{0,1:T(8,128)(2,1)}, bf16[3,1024]{0,1:T(8,128)(2,1)}, u32[]{:S(2)}, u32[]{:S(2)}) collective-permute-start(bf16[3,1024]{0,1:T(8,128)(2,1)} %get-tuple-element.661), channel_id=1, source_target_pairs={{0,4},{4,8},{8,12},{12,16},{16,20},{20,24},{24,28},{1,5},{5,9},{9,... | collective-permute-start | bytes 18440 | tf_op jit(solution)/shard_map/ppermute | solution.py:19
  76.1 1.6 maximum_convert_fusion
  77.8 5.7 %multiply_convert_fusion.8 = (bf16[512,1024]{0,1:T(8,128)(2,1)}, bf16[512,1024]{0,1:T(8,128)(2,1)}) fusion(f32[518,1024]{0,1:T(8,128)S(1)} %maximum_convert_fusion, f32[1024]{0:T(1024)S(1)} %bitcast.314, f32[1024]{0:T(1024)S(1)} %bitcast.315, f32[1024]{0:T(1024)S(1)} %bitcast.316, f32[1024]{0:T(1024)S(1)} %bitcast.311, f32[1024]{0:T(1024)S(1)} %bitcast.317, ...), kind=kLoop, calls=%fused_computation.123 | loop fusion | flops 12582912 | bytes 16809984 | tf_op jit(solution)/shard_map/convert_element_type | solution.py:115
  83.5 2.5 rev.20
  86.0 1.3 copy_bitcast_fusion.1
  87.3 1.7 broadcast.56.clone
  88.9 1.6 broadcast.58.clone
  90.5 20.3 %while.74 = (s32[]{:T(128)}, f32[16,64,128]{2,1,0:T(8,128)S(1)}, f32[16]{0:T(128)S(1)}, f32[4,128,16,64]{1,3,2,0:T(8,128)}, f32[4,128,16]{2,1,0:T(8,128)S(1)}, /...) while((s32[]{:T(128)}, f32[16,64,128]{2,1,0:T(8,128)S(1)}, ...), condition=%wide.region_7.8_spmd.clone, body=%wide.region_5.7_spmd.clone.sunk | while | flops 73816096 | bytes 3699580 | solution.py:86
  91.6 1.2 convolution_add_fusion.5
  93.2 2.3 fusion.195
  96.7 1.2 convolution_add_fusion.5
  98.2 2.4 fusion.195
  101.8 1.2 convolution_add_fusion.5
  103.3 2.4 fusion.195
  106.9 1.2 convolution_add_fusion.5
  108.4 2.4 fusion.195
  111.5 1.3 reshape_reshape.3
  112.9 1.3 copy.82
  115.1 1.7 broadcast.56.clone.1
  116.8 1.6 broadcast.58.clone.1
  118.3 23.3 %while.72 = (s32[]{:T(128)}, f32[16,64,128]{2,1,0:T(8,128)S(1)}, f32[16]{0:T(128)S(1)}, f32[4,128,16,64]{1,3,2,0:T(8,128)}, f32[4,128,16]{2,1,0:T(8,128)S(1)}, /...) while((s32[]{:T(128)}, f32[16,64,128]{2,1,0:T(8,128)S(1)}, ...), condition=%wide.region_2.3_spmd.clone, body=%wide.region_0.2_spmd.clone.sunk | while | flops 73816096 | bytes 3699580 | solution.py:86
  119.5 1.2 convolution_add_fusion.4
  121.8 2.3 fusion.185
  125.3 1.2 convolution_add_fusion.4
  127.6 2.3 fusion.185
  131.1 1.2 convolution_add_fusion.4
  133.4 2.3 fusion.185
  137.0 1.2 convolution_add_fusion.4
  139.3 2.3 fusion.185
  142.5 1.2 dynamic-slice
  145.7 13.0 %all-reduce.2 = (bf16[128]{0:T(256)(128)(2,1)S(1)}, bf16[128]{0:T(256)(128)(2,1)S(1)}) all-reduce(bf16[128]{0:T(256)(128)(2,1)S(1)} %dynamic-update-slice.1, bf16[128]{0:T(256)(128)(2,1)S(1)} %dynamic-update-slice), channel_id=4, replica_groups=mesh['frame'=8,'row'=4] {'frame'}, use_global_device_ids=true, to_apply=%add.1 | all-reduce | flops 256 | bytes 1024
  159.8 9.2 %while.75 = (s32[]{:T(128)}, f32[16,64,128]{2,1,0:T(8,128)S(1)}, s32[]{:T(128)}, bf16[8,16]{1,0:T(8,128)(2,1)S(1)}, bf16[8,16,64,128]{3,2,1,0:T(8,128)(2,1)}, /*index=5*/s32[]{:T(128)}, s32[]{:T(128)}, s32[]{:T(128)}, s32[]{:T(128)}) while((s32[]{:T(128)}, f32[16,64,128]{2,1,0:T(8,128)S(1)}, s32[]{:T(128)}, ...), condition=%wide.region_9.10_spmd.clone, body=%wide.region_8.9_spmd.clone.sunk | while | flops 655384 | bytes 1311055 | solution.py:46
  159.8 1.1 fusion.196
  161.0 1.1 fusion.196
  162.2 1.1 fusion.196
  163.3 1.1 fusion.196
  164.4 1.1 fusion.196
  165.6 1.1 fusion.196
  166.8 1.1 fusion.196
  167.9 1.1 fusion.196
  169.0 2.9 %add_bitcast_fusion = f32[4,16,8,8,128]{4,3,2,1,0:T(8,128)S(1)} fusion(f32[4,128,16,64]{1,3,2,0:T(8,128)} %get-tuple-element.372, f32[4,16,64,128]{3,2,1,0:T(8,128)} %get-tuple-element.373, f32[16]{0:T(128)S(1)} %get-tuple-element.674, f32[4,128,16]{1,2,0:T(8,128)S(1)} %copy.94, f32[16,64,128]{2,1,0:T(8,128)S(1)} %get-tuple-element.377, ...), kind=kOutput, calls=%fused_computation.118 | convolution fusion | flops 138412032 | bytes 8028480 | tf_op jit(solution)/shard_map/btn,bhpn->bthp/dot_general | solution.py:94
  171.9 1.7 copy.122
  173.6 4.2 %rev.23 = f32[512,16,64]{0,2,1:T(8,128)} reverse(f32[512,16,64]{0,2,1:T(8,128)} %bitcast.294), dimensions={0} | reverse | bytes 4194304 | tf_op jit(solution)/shard_map/jit(_flip)/rev | solution.py:190
  177.8 9.2 %while.73 = (s32[]{:T(128)}, f32[16,64,128]{2,1,0:T(8,128)S(1)}, s32[]{:T(128)}, bf16[8,16]{1,0:T(8,128)(2,1)S(1)}, bf16[8,16,64,128]{3,2,1,0:T(8,128)(2,1)}, /*index=5*/s32[]{:T(128)}, s32[]{:T(128)}) while((s32[]{:T(128)}, f32[16,64,128]{2,1,0:T(8,128)S(1)}, s32[]{:T(128)}, bf16[8,16]{1,0:T(8,128)(2,1)S(1)}, ...), condition=%wide.region_4.5_spmd.clone, body=%wide.region_3.4_spmd.clone.sunk | while | flops 655380 | bytes 1310993 | solution.py:46
  177.9 1.2 fusion.186
  179.1 1.1 fusion.186
  180.2 1.1 fusion.186
  182.5 1.1 fusion.186
  187.1 3.0 %add_bitcast_fusion.1 = f32[4,16,8,8,128]{4,3,2,1,0:T(8,128)S(1)} fusion(f32[4,128,16,64]{1,3,2,0:T(8,128)} %get-tuple-element.365, f32[4,16,64,128]{3,2,1,0:T(8,128)} %get-tuple-element.366, f32[16]{0:T(128)S(1)} %get-tuple-element.673, f32[4,128,16]{1,2,0:T(8,128)S(1)} %copy.86, f32[16,64,128]{2,1,0:T(8,128)S(1)} %get-tuple-element.370, ...), kind=kOutput, calls=%fused_computation.121 | convolution fusion | flops 138412032 | bytes 8028480 | tf_op jit(solution)/shard_map/btn,bhpn->bthp/dot_general | solution.py:94
  190.4 3.2 %multiply_reduce_fusion = (f32[512]{0:T(512)S(1)}, f32[512,1024]{0,1:T(8,128)}) fusion(bf16[512,2592]{0,1:T(8,128)(2,1)} %bitcast.302, f32[512,16,64]{0,2,1:T(8,128)S(1)} %bitcast_add_fusion), kind=kLoop, calls=%fused_computation.117 | loop fusion | flops 4193792 | bytes 5244928 | tf_op jit(solution)/shard_map/reduce_sum | solution.py:193
  193.6 8.3 %psum.7 = f32[512]{0:T(512)S(1)} all-reduce(f32[512]{0:T(512)S(1)} %get-tuple-element.647), channel_id=1, replica_groups=mesh['frame'=8,'row'=4] {'row'}, use_global_device_ids=true, to_apply=%region_11.12 | all-reduce | flops 512 | bytes 4096 | tf_op jit(solution)/shard_map/psum | solution.py:194
  202.0 6.8 %fusion.58 = bf16[512,1,2048]{2,0,1:T(8,128)(2,1)} fusion(bf16[1024,2048]{1,0:T(8,128)(2,1)} %param.29, f32[512,1024]{0,1:T(8,128)} %get-tuple-element.648, f32[1024]{0:T(1024)S(1)} %copy-done.27, f32[512]{0:T(512)S(1)} %add_rsqrt_fusion), kind=kOutput, calls=%fused_computation.85 | convolution fusion | flops 2150105088 | bytes 8394752 | tf_op jit(solution)/shard_map/fpc,cd->fpd/dot_general | solution.py:198
  208.8 42.8 %reduce-scatter.2.cloned.1.call-done = bf16[128,1,2048]{2,0,1:T(8,128)(2,1)} async-done(((bf16[512,1,2048]{2,0,1:T(8,128)(2,1)}), bf16[128,1,2048]{2,0,1:T(8,128)(2,1)}) %reduce-scatter.2.cloned.1.call-update) | async-done | bytes 524304 | tf_op jit(solution)/shard_map/reduce_scatter | solution.py:199
  (254 shorter events, 35.4 us)
Async XLA Ops:
  6.5 56.2 %copy-start = (bf16[2048,512]{1,0:T(8,128)(2,1)S(1)}, bf16[2048,512]{1,0:T(8,128)(2,1)}, u32[]{:S(2)}) copy-start(bf16[2048,512]{1,0:T(8,128)(2,1)} %param.22) | copy-start | bytes 6291460
  6.5 153.3 %all-gather.9.cloned.1.call-start = ((), (), s32[]{:S(2)}) async-start(), calls=%async_computation.3 | async-start | bytes 2359296 | tf_op jit(solution)/shard_map/all_gather | solution.py:28
  6.5 17.2 %collective-permute-start = (bf16[1,128,2048]{2,1,0:T(8,128)(2,1)}, bf16[1,128,2048]{2,1,0:T(8,128)(2,1)S(1)}, u32[]{:S(2)}, u32[]{:S(2)}) collective-permute-start(bf16[1,128,2048]{2,1,0:T(8,128)(2,1)} %param.19), channel_id=1, source_target_pairs={{0,1},{1,2},{2,3},{3,0},{4,5},{5,6},{6,7},{7,4},{8,9},{9,10},{10,1... | collective-permute-start | bytes 1572872 | tf_op jit(solution)/shard_map/ppermute | solution.py:137
  23.7 15.8 %copy-start.7 = (bf16[1,128,2048]{2,1,0:T(8,128)(2,1)}, bf16[1,128,2048]{2,1,0:T(8,128)(2,1)S(1)}, u32[]{:S(2)}) copy-start(bf16[1,128,2048]{2,1,0:T(8,128)(2,1)S(1)} %collective-permute-done) | copy-start | bytes 1572868
  23.8 15.0 %collective-permute-start.1 = (bf16[1,128,2048]{2,1,0:T(8,128)(2,1)S(1)}, bf16[1,128,2048]{2,1,0:T(8,128)(2,1)}, u32[]{:S(2)}, u32[]{:S(2)}) collective-permute-start(bf16[1,128,2048]{2,1,0:T(8,128)(2,1)S(1)} %collective-permute-done), channel_id=1, source_target_pairs={{0,1},{1,2},{2,3},{3,0},{4,5},{5,6},{6,7},{7,4},{8,9},{9,10},{10,1... | collective-permute-start | bytes 1572872 | tf_op jit(solution)/shard_map/ppermute | solution.py:137
  38.7 14.3 %collective-permute-start.2 = (bf16[1,128,2048]{2,1,0:T(8,128)(2,1)}, bf16[1,128,2048]{2,1,0:T(8,128)(2,1)}, u32[]{:S(2)}, u32[]{:S(2)}) collective-permute-start(bf16[1,128,2048]{2,1,0:T(8,128)(2,1)} %collective-permute-done.1), channel_id=1, source_target_pairs={{0,1},{1,2},{2,3},{3,0},{4,5},{5,6},{6,7},{7,4},{8,9},{9,10},{10,1... | collective-permute-start | bytes 1572872 | tf_op jit(solution)/shard_map/ppermute | solution.py:137
  39.5 15.7 %copy-start.8 = (bf16[1,128,2048]{2,1,0:T(8,128)(2,1)S(1)}, bf16[1,128,2048]{2,1,0:T(8,128)(2,1)}, u32[]{:S(2)}) copy-start(bf16[1,128,2048]{2,1,0:T(8,128)(2,1)} %copy-done.7) | copy-start | bytes 1572868
  39.5 15.8 %copy-start.6 = (bf16[1,128,2048]{2,1,0:T(8,128)(2,1)S(1)}, bf16[1,128,2048]{2,1,0:T(8,128)(2,1)}, u32[]{:S(2)}) copy-start(bf16[1,128,2048]{2,1,0:T(8,128)(2,1)} %param.19) | copy-start | bytes 1572868
  55.3 2.6 %copy-start.25 = (bf16[2048,1024]{1,0:T(8,128)(2,1)S(1)}, bf16[2048,1024]{1,0:T(8,128)(2,1)}, u32[]{:S(2)}) copy-start(bf16[2048,1024]{1,0:T(8,128)(2,1)} %param.20) | copy-start | bytes 12582916
  57.9 2.4 copy-start.26
  62.8 1.3 copy-start.15
  65.4 6.9 %copy-start.5 = (bf16[1,512,2592]{1,2,0:T(8,128)(2,1)}, bf16[1,512,2592]{1,2,0:T(8,128)(2,1)S(1)}, u32[]{:S(2)}) copy-start(bf16[1,512,2592]{1,2,0:T(8,128)(2,1)S(1)} %fusion.115) | copy-start | bytes 7962628
  67.1 8.9 %collective-permute-start.4 = (bf16[3,1024]{0,1:T(8,128)(2,1)}, bf16[3,1024]{0,1:T(8,128)(2,1)}, u32[]{:S(2)}, u32[]{:S(2)}) collective-permute-start(bf16[3,1024]{0,1:T(8,128)(2,1)} %get-tuple-element.662), channel_id=1, source_target_pairs={{4,0},{8,4},{12,8},{16,12},{20,16},{24,20},{28,24},{5,1},{9,5},{13... | collective-permute-start | bytes 18440 | tf_op jit(solution)/shard_map/ppermute | solution.py:20
  68.4 7.6 %collective-permute-start.3 = (bf16[3,1024]{0,1:T(8,128)(2,1)}, bf16[3,1024]{0,1:T(8,128)(2,1)}, u32[]{:S(2)}, u32[]{:S(2)}) collective-permute-start(bf16[3,1024]{0,1:T(8,128)(2,1)} %get-tuple-element.661), channel_id=1, source_target_pairs={{0,4},{4,8},{8,12},{12,16},{16,20},{20,24},{24,28},{1,5},{5,9},{9,... | collective-permute-start | bytes 18440 | tf_op jit(solution)/shard_map/ppermute | solution.py:19
  73.9 1.3 copy-start.11
  75.2 2.5 copy-start.9
  76.0 1.7 copy-start.16
  76.0 1.7 copy-start.17
  76.0 1.7 copy-start.18
  76.0 1.7 copy-start.19
  76.0 1.7 copy-start.20
  76.0 1.7 copy-start.21
  87.2 3.3 %copy-start.23 = (f32[16]{0:T(128)S(1)}, f32[16]{0:T(128)}, u32[]{:S(2)}) copy-start(f32[16]{0:T(128)} %custom-call.4) | copy-start | bytes 196
  110.8 0.7 copy-start.13
  112.9 3.9 %copy-start.2 = (bf16[4,128,16,64]{1,0,3,2:T(4,128)(2,1)}, bf16[4,128,16,64]{1,0,3,2:T(4,128)(2,1)S(1)}, u32[]{:S(2)}) copy-start(bf16[4,128,16,64]{1,0,3,2:T(4,128)(2,1)S(1)} %reshape_reshape.3) | copy-start | bytes 3145732
  115.0 62.8 %all-gather.7.cloned.1.call-start = ((), (), s32[]{:S(2)}) async-start(), calls=%async_computation.2 | async-start | bytes 2359296 | tf_op jit(solution)/shard_map/all_gather | solution.py:28
  115.0 3.3 %copy-start.22 = (f32[16]{0:T(128)S(1)}, f32[16]{0:T(128)}, u32[]{:S(2)}) copy-start(f32[16]{0:T(128)} %custom-call.1) | copy-start | bytes 196
  118.3 26.8 %copy-start.14 = (f32[4,128,16]{2,1,0:T(8,128)S(1)}, f32[4,128,16]{2,1,0:T(8,128)}, u32[]{:S(2)}) copy-start(f32[4,128,16]{2,1,0:T(8,128)} %copy-done.13) | copy-start | bytes 98308
  141.7 0.8 copy-start.24
  142.4 109.2 %reduce-scatter.2.cloned.1.call-start = ((), (), s32[]{:S(2)}) async-start(), calls=%async_computation.1 | async-start | bytes 2621440 | tf_op jit(solution)/shard_map/reduce_scatter | solution.py:199
  159.8 9.2 %copy-start.12 = (bf16[4,128,128]{1,0,2:T(4,128)(2,1)S(1)}, bf16[4,128,128]{1,0,2:T(4,128)(2,1)}, u32[]{:S(2)}) copy-start(bf16[4,128,128]{1,0,2:T(4,128)(2,1)} %copy-done.11) | copy-start | bytes 393220
  177.8 9.2 %copy-start.3 = (bf16[4,128,16,64]{1,0,3,2:T(4,128)(2,1)S(1)}, bf16[4,128,16,64]{1,0,3,2:T(4,128)(2,1)}, u32[]{:S(2)}) copy-start(bf16[4,128,16,64]{1,0,3,2:T(4,128)(2,1)} %copy-done.2) | copy-start | bytes 3145732
  177.8 9.2 %copy-start.10 = (bf16[4,128,128]{1,0,2:T(4,128)(2,1)S(1)}, bf16[4,128,128]{1,0,2:T(4,128)(2,1)}, u32[]{:S(2)}) copy-start(bf16[4,128,128]{1,0,2:T(4,128)(2,1)} %copy-done.9) | copy-start | bytes 393220
  187.1 3.0 %copy-start.4 = (f32[512,16,64]{0,2,1:T(8,128)S(1)}, f32[512,16,64]{0,2,1:T(8,128)}, u32[]{:S(2)}) copy-start(f32[512,16,64]{0,2,1:T(8,128)} %rev.23) | copy-start | bytes 6291460
  190.4 11.6 %copy-start.27 = (f32[1024]{0:T(1024)S(1)}, f32[1024]{0:T(1024)}, u32[]{:S(2)}) copy-start(f32[1024]{0:T(1024)} %param.28) | copy-start | bytes 12292
  202.0 49.7 %copy-start.1 = (bf16[2048,512]{1,0:T(8,128)(2,1)S(1)}, bf16[2048,512]{1,0:T(8,128)(2,1)}, u32[]{:S(2)}) copy-start(bf16[2048,512]{1,0:T(8,128)(2,1)} %param.22) | copy-start | bytes 6291460
Sparse Core Ops, SparseCore 0:
  115.1 26.5 all-gather.8
  143.6 27.7 all-gather.6
  209.0 42.6 reduce-scatter.1
